TPU v7x, 256 devices: a whole 4x4x8 slice. The times are simulated.
256 devices in a mesh: grp: 4 (over z_hi), dev: 64 (over y, x, z_lo, core).
Axes of the slice: x: 4, y: 4, z: 8 (z_hi: 4, z_lo: 2; z = z_hi * 2 + z_lo), core: 2. Of those that a mesh axis runs over, the one named last changes fastest.
Arguments:
- amounts: float32 [64, 4194304], P('dev', 'grp'), may hold values from -0.06 to 0.06, as said below
Outputs:
- offsets: float32 [64, 4194304], P(None, ('grp', 'dev'))
Inputs may be any that keep to these rules, and one draw needn't show every extreme that they name: `amounts`: each entry lies within 0.06 of zero.
All inputs are finite; a program needn't handle non-finite values.
Results may differ from a plain program's by a relative error of at most 0.00095.
Values sent between devices are 32-bit elements; how exact they have to be, the bound alone decides.
A program may use at most 64 MiB of HBM per device.

v0:
```python
import jax
import jax.numpy as jnp
from jax import lax
from jax.sharding import PartitionSpec as P


def copy_for_each(array, axis):
    copies = jnp.broadcast_to(array, (lax.axis_size(axis), *array.shape))
    return lax.all_to_all(copies, axis, split_axis=0, concat_axis=0, tiled=True)


def joined_by_halves(pieces, combine):
    while len(jax.tree.leaves(pieces)[0]) > 1:
        pieces = jax.vmap(combine)(*(pieces[side::2] for side in (0, 1)))
    return pieces[0]


def prefix(array, axis, combine, identity):
    devices, position = (lax.axis_size(axis), lax.axis_index(axis))
    passed = jnp.arange(devices) < position

    def kept(part, zero, own):
        part = jnp.where(
            passed.reshape(-1, *(1 for _ in own.shape)), part, jnp.asarray(zero, own.dtype)
        )
        return part

    pieces = copy_for_each(array, axis)
    return joined_by_halves(kept(pieces, identity, array), combine)


def local_scan(values):
    chans, length = values.shape
    block_len = 512
    count = length // block_len
    row_index = lax.broadcasted_iota(jnp.int32, (block_len, block_len), 0)
    col_index = lax.broadcasted_iota(jnp.int32, (block_len, block_len), 1)
    upper_ones = (row_index < col_index).astype(jnp.float32)
    blocks = values.reshape(chans * count, block_len)
    within = jnp.dot(
        blocks, upper_ones, precision=lax.Precision.HIGHEST, preferred_element_type=jnp.float32
    )
    within = within.reshape(chans, count, block_len)
    sums = jnp.sum(values.reshape(chans, count, block_len), axis=2)
    starts = jnp.cumsum(sums, axis=1) - sums
    result = (within + starts[:, :, None]).reshape(chans, length)
    return (result, jnp.sum(sums, axis=1))


def combine(earlier, later):
    return earlier + later


def relayout(values):
    return lax.all_to_all(values, "dev", split_axis=1, concat_axis=0, tiled=True)


def chain_groups(column_sum):
    return prefix(column_sum, "grp", combine, jnp.zeros_like(column_sum))


def local(amounts):
    partial_sums, column_sum = local_scan(amounts)
    result = relayout(partial_sums + chain_groups(column_sum)[:, None])
    return result


def solution(mesh):
    return jax.shard_map(
        local,
        mesh=mesh,
        in_specs=(P("dev", "grp"),),
        out_specs=P(None, ("grp", "dev")),
        check_vma=False,
    )
```

profile of v0, /device:TPU:1, one launch (start us, length us, event | category | flops | bytes accessed | tf_op | source)
XLA Modules:
  0.0 148.6 jit_solution(3363401355995021903)
XLA Ops:
  0.0 0.6 broadcast.51
  0.6 40.4 %fusion.3 = (f32[]{:T(128)}, f32[1048576]{0:T(1024)}) fusion(f32[1,1048576]{1,0:T(1,128)} %param.1, f32[]{:T(128)} %broadcast.51), kind=kLoop, calls=%fused_computation.9 | loop fusion | flops 1048575 | bytes 8388616 | tf_op jit(solution)/shard_map/reduce_sum | solution.py:47
  41.0 1.3 broadcast_in_dim.8
  42.3 9.0 %all-to-all-start = ((f32[4,1,1]{2,1,0:T(1,128)}), f32[4,1,1]{2,1,0:T(1,128)S(1)}, u32[]{:S(2)}, u32[]{:S(2)}) async-start(f32[4,1,1]{2,1,0:T(1,128)} %broadcast_in_dim.8), calls=%async_computation | async-start | bytes 4096 | tf_op jit(solution)/shard_map/all_to_all | solution.py:9
  51.3 4.9 %reshape.103 = f32[2048,512]{1,0:T(8,128)} reshape(f32[1048576]{0:T(1024)} %get-tuple-element.6) | data formatting | bytes 8388608 | tf_op jit(solution)/shard_map/reshape | solution.py:39
  56.2 2.5 %reduce_sum.18 = f32[2048]{0:T(1024)S(1)} reduce(f32[2048,512]{1,0:T(8,128)} %reshape.103, f32[]{:T(128)} %constant.10.clone.1), dimensions={1}, to_apply=%region_0.0 | reduce | flops 1046528 | bytes 4202500 | tf_op jit(solution)/shard_map/reduce_sum | solution.py:44
  58.7 0.3 reduce-window.6
  59.0 0.2 slice_reduce_fusion
  59.2 0.2 reduce-window.9
  59.4 0.1 broadcast.45
  59.5 0.0 all-to-all-done
  59.5 0.1 reduce.7
  59.6 0.1 slice.23
  59.7 0.1 slice.22
  59.8 0.6 fusion.4
  61.7 8.6 %add_bitcast_fusion = f32[2048,512]{0,1:T(8,128)} fusion(f32[2048,512]{1,0:T(8,128)} %reshape.103, f32[]{:T(128)} %bitcast.4, f32[2048]{0:T(1024)S(1)} %fusion.2), kind=kOutput, calls=%fused_computation.1 | convolution fusion | flops 6445072384 | bytes 8396804 | tf_op jit(solution)/shard_map/dot_general | solution.py:40
  70.3 5.3 %copy.5 = f32[2048,512]{1,0:T(8,128)} copy(f32[2048,512]{0,1:T(8,128)} %add_bitcast_fusion) | data formatting | bytes 8388608 | tf_op jit(solution)/shard_map/add | solution.py:64
  75.6 7.6 %add.50 = f32[1,64,16384]{2,0,1:T(1,128)} reshape(f32[2048,512]{1,0:T(8,128)} %copy.5) | data formatting | bytes 8388608 | tf_op jit(solution)/shard_map/add | solution.py:64
  83.3 60.9 %all_to_all.22 = f32[1,64,16384]{2,0,1:T(1,128)S(1)} all-to-all(f32[1,64,16384]{2,0,1:T(1,128)} %add.50), channel_id=1, replica_groups=mesh['grp'=4,'dev'=64] {'dev'}, dimensions={1} | all-to-all | bytes 8388608 | tf_op jit(solution)/shard_map/all_to_all | solution.py:55
  144.2 4.4 %copy.9 = f32[1,64,16384]{2,1,0:T(8,128)} copy(f32[1,64,16384]{2,0,1:T(1,128)S(1)} %all_to_all.22) | data formatting | bytes 8388608
  (4 shorter events, 0.0 us)
Async XLA Ops:
  42.3 17.2 %all-to-all-start = ((f32[4,1,1]{2,1,0:T(1,128)}), f32[4,1,1]{2,1,0:T(1,128)S(1)}, u32[]{:S(2)}, u32[]{:S(2)}) async-start(f32[4,1,1]{2,1,0:T(1,128)} %broadcast_in_dim.8), calls=%async_computation | async-start | bytes 4096 | tf_op jit(solution)/shard_map/all_to_all | solution.py:9
where the time goes:
time: 149 us
  blocking collectives  60.9 us (41%)
  other arithmetic  43.5 us (29%)
  local copies, waits for them, and re-layouts  25.2 us (17%)
  starting transfers between devices  9 us (6%)
  matrix products  8.61 us (6%)
    all_to_all x1, blocking collectives, relayout(): lax.all_to_all(values, 'dev', split_axis=1, concat_axis=0, tiled=True)  60.9 us
    reduce_sum x1, other arithmetic, local_scan(): return (result, jnp.sum(sums, axis=1))  40.4 us
    add x2, local copies, waits for them, and re-layouts, local(): result = relayout(partial_sums + chain_groups(column_sum)[:, None])  13 us
    all_to_all x1, starting transfers between devices, copy_for_each(): return lax.all_to_all(copies, axis, split_axis=0, concat_axis=0, tiled=True)  9 us
    dot_general x1, matrix products, local_scan(): jnp.dot(blocks, upper_ones, precision=lax.Precision.HIGHEST, preferred_el...  8.61 us
    unnamed x2, local copies, waits for them, and re-layouts  4.98 us
    reshape x1, local copies, waits for them, and re-layouts, local_scan(): blocks = values.reshape(chans * count, block_len)  4.92 us
  transfers between devices with their start and end apart: 1, of which 0 were waited for; matrix products, arithmetic and copies ran while one was open for 6% of the time, Pallas kernels for 0%

commit v1 on v0

v1 whole, which is shorter than its diff:
```python
import jax
import jax.numpy as jnp
from jax import lax
from jax.experimental import pallas as pl
from jax.experimental.pallas import tpu as pltpu
from jax.sharding import PartitionSpec as P

MESH = pl.DeviceIdType.MESH
LANES = 128
ROWS = 128
N = 64
GROUPS = 4
SPLIT = 2
FIRST = 16


def send_order():
    order = []
    for k in range(N // 2):
        j = (13 * k) % (N // 2)
        for s in range(2):
            order.append(((j // 8 + 2 * s) % 4, ((j // 2) % 4 + 2 * s) % 4, s, j % 2))
    return order[1:]


def split3(v):
    hi = v.astype(jnp.bfloat16)
    rest = v - hi.astype(jnp.float32)
    mid = rest.astype(jnp.bfloat16)
    lo = (rest - mid.astype(jnp.float32)).astype(jnp.bfloat16)
    return hi, mid, lo


def dot(a, b):
    return jnp.dot(a, b, preferred_element_type=jnp.float32)


def gather_kernel(
    x_hbm, buf, xv, lane_w, row_w, part, st, srecv, tot, trecv,
    load_sem, send_sem, recv_sem, small_send, small_recv, tot_send, tot_recv,
):
    me = lax.axis_index("dev")
    grp = lax.axis_index("grp")
    y, x, z, c = me // 16, (me // 4) % 4, (me // 2) % 2, me % 2

    def remote(src, dst, ssem, rsem, dev):
        return pltpu.make_async_remote_copy(
            src_ref=src, dst_ref=dst, send_sem=ssem, recv_sem=rsem,
            device_id={"dev": dev}, device_id_type=MESH,
        )

    load = pltpu.make_async_copy(x_hbm, xv, load_sem)
    load.start()
    barrier = pltpu.get_barrier_semaphore()

    def greet(i, _):
        pl.semaphore_signal(barrier, inc=1, device_id={"dev": (me + i) % N}, device_id_type=MESH)
        return 0

    lax.fori_loop(1, N, greet, 0)
    for i in range(1, GROUPS):
        pl.semaphore_signal(
            barrier, inc=1, device_id={"grp": (grp + i) % GROUPS}, device_id_type=MESH
        )

    r = lax.broadcasted_iota(jnp.int32, (2 * LANES, 2 * LANES), 0) % LANES
    q = lax.broadcasted_iota(jnp.int32, (2 * LANES, 2 * LANES), 1)
    lane_w[...] = ((r < q) | (q >= LANES)).astype(jnp.float32).astype(jnp.bfloat16)
    r = lax.broadcasted_iota(jnp.int32, (ROWS, 2 * ROWS), 0)
    q = lax.broadcasted_iota(jnp.int32, (ROWS, 2 * ROWS), 1) % ROWS
    row_w[...] = (q < r).astype(jnp.float32).astype(jnp.bfloat16)

    pl.semaphore_wait(barrier, N - 1 + GROUPS - 1)

    def send(o):
        t = ((y + o[0]) % 4) * 16 + ((x + o[1]) % 4) * 4 + ((z + o[2]) % 2) * 2 + (c + o[3]) % 2
        h = ROWS // SPLIT
        for i in range(SPLIT):
            remote(
                x_hbm.at[t, pl.ds(i * h, h)], buf.at[me, pl.ds(i * h, h)],
                send_sem, recv_sem.at[me], t,
            ).start()

    order = send_order()
    for o in order[:FIRST]:
        send(o)

    load.wait()

    def range_sum(t, _):
        part[t] = jnp.sum(xv[t].reshape(ROWS // 8, 8, LANES), axis=0)
        return 0

    lax.fori_loop(0, N, range_sum, 0)
    sums = jnp.sum(jnp.sum(part[...], axis=1), axis=1, keepdims=True)
    sums = jnp.broadcast_to(sums, (N, LANES))
    tot[...] = jnp.broadcast_to(jnp.sum(sums, axis=0, keepdims=True), (8, LANES))
    low = row_w[0:N, 0:N]
    a, b, d = split3(sums)
    pre = dot(low, a) + dot(low, b) + dot(low, d)
    trecv[grp] = jnp.zeros((8, LANES), jnp.float32)
    copies = []
    for i in range(1, GROUPS):
        copy = pltpu.make_async_remote_copy(
            src_ref=tot, dst_ref=trecv.at[grp], send_sem=tot_send, recv_sem=tot_recv,
            device_id={"grp": (grp + i) % GROUPS}, device_id_type=MESH,
        )
        copy.start()
    pltpu.make_async_copy(trecv.at[pl.ds(0, 3)], trecv.at[pl.ds(0, 3)], tot_send).wait()
    pltpu.make_async_copy(trecv.at[pl.ds(0, 3)], trecv.at[pl.ds(0, 3)], tot_recv).wait()
    base = jnp.zeros((8, LANES), jnp.float32)
    for i in range(GROUPS - 1):
        base = base + jnp.where(i < grp, trecv[i], 0.0)
    st[...] = pre + base[0:1]

    for o in order:
        t = ((y + o[0]) % 4) * 16 + ((x + o[1]) % 4) * 4 + ((z + o[2]) % 2) * 2 + (c + o[3]) % 2
        remote(st.at[pl.ds(t, 1)], srecv.at[pl.ds(me, 1)], small_send, small_recv, t).start()
    for o in order[FIRST:]:
        send(o)

    def scanned(v, start):
        hi, mid, lo = split3(v)
        both = dot(jnp.concatenate([hi, mid], axis=1), lane_w[...]) + dot(lo, lane_w[0:LANES])
        a, b, d = split3(both[:, LANES:])
        rows = dot(row_w[...], jnp.concatenate([a, b], axis=0)) + dot(row_w[:, 0:ROWS], d)
        return both[:, :LANES] + (rows + start)

    buf[me] = scanned(xv[me], st[pl.ds(me, 1)])
    pltpu.make_async_copy(st.at[pl.ds(0, N - 1)], srecv.at[pl.ds(0, N - 1)], small_recv).wait()

    def receive(i, _):
        k, s = i // 2, i % 2
        j = (13 * k) % (N // 2)
        src = (
            ((y + 8 - j // 8 - 2 * s) % 4) * 16 + ((x + 8 - (j // 2) % 4 - 2 * s) % 4) * 4
            + ((z + s) % 2) * 2 + (c + j) % 2
        )
        pltpu.make_async_copy(buf.at[src], buf.at[src], recv_sem.at[src]).wait()
        buf[src] = scanned(buf[src], srecv[pl.ds(src, 1)])
        return 0

    lax.fori_loop(1, N, receive, 0)
    pltpu.make_async_copy(st.at[pl.ds(0, N - 1)], srecv.at[pl.ds(0, N - 1)], small_send).wait()
    pltpu.make_async_copy(buf.at[pl.ds(0, N - 1)], buf.at[pl.ds(0, N - 1)], send_sem).wait()


def place_kernel(buf, out, sem):
    for t in range(N):
        pltpu.make_async_copy(buf.at[t], out.at[t // 8, :, t % 8], sem).start()
    pltpu.make_async_copy(buf, buf, sem).wait()


def local(amounts):
    slabs = amounts.reshape(N, ROWS, LANES)
    f32, bf16, dma = jnp.float32, jnp.bfloat16, pltpu.SemaphoreType.DMA
    buf = pl.pallas_call(
        gather_kernel,
        out_shape=pltpu.VMEM((N, ROWS, LANES), f32),
        in_specs=[pl.BlockSpec(memory_space=pltpu.HBM)],
        out_specs=pl.BlockSpec(memory_space=pltpu.VMEM),
        scratch_shapes=[
            pltpu.VMEM((N, ROWS, LANES), f32),
            pltpu.VMEM((2 * LANES, 2 * LANES), bf16),
            pltpu.VMEM((ROWS, 2 * ROWS), bf16),
            pltpu.VMEM((N, 8, LANES), f32),
            pltpu.VMEM((N, LANES), f32),
            pltpu.VMEM((N, LANES), f32),
            pltpu.VMEM((8, LANES), f32),
            pltpu.VMEM((GROUPS, 8, LANES), f32),
            dma, dma, dma((N,)), dma, dma, dma, dma,
        ],
        compiler_params=pltpu.CompilerParams(
            collective_id=0, has_side_effects=True, vmem_limit_bytes=56 * 2**20
        ),
    )(slabs)
    out = pl.pallas_call(
        place_kernel,
        out_shape=jax.ShapeDtypeStruct((8, ROWS, 8, LANES), f32),
        in_specs=[pl.BlockSpec(memory_space=pltpu.VMEM)],
        out_specs=pl.BlockSpec(memory_space=pltpu.HBM),
        scratch_shapes=[dma],
        compiler_params=pltpu.CompilerParams(vmem_limit_bytes=8 * 2**20),
    )(pltpu.with_memory_space_constraint(buf, pltpu.VMEM))
    return out.transpose(0, 2, 1, 3).reshape(N, ROWS * LANES)


def solution(mesh):
    return jax.shard_map(
        local,
        mesh=mesh,
        in_specs=(P("dev", "grp"),),
        out_specs=P(None, ("grp", "dev")),
        check_vma=False,
    )
```

time: 149 us -> 76.4 us (0.51)
  the two profiles are of different devices: /device:TPU:1 before, /device:TPU:41 now
where the time goes in v1:
time: 76.4 us
  Pallas kernels  76.4 us (100%)
    pallas_call x1, Pallas kernels, local(): pl.pallas_call(gather_kernel, out_shape=pltpu.VMEM((N, ROWS, LANES), f32)...  74.4 us
    pallas_call x1, Pallas kernels, local(): pl.pallas_call(place_kernel, out_shape=jax.ShapeDtypeStruct((8, ROWS, 8,...  1.97 us

profile of v1, /device:TPU:41, one launch (start us, length us, event | category | flops | bytes accessed | tf_op | source)
XLA Modules:
  0.0 76.4 jit_solution(6801528979773327155)
XLA Ops:
  0.0 74.4 %shard_map.17.buf = f32[64,128,128]{2,1,0:T(8,128)S(1)} custom-call(f32[64,128,128]{2,1,0:T(8,128)} %bitcast.4), custom_call_target="tpu_custom_call" | custom-call | tf_op jit(solution)/shard_map/pallas_call | solution.py:157
  74.4 2.0 %shard_map.18 = f32[8,128,8,128]{3,2,1,0:T(8,128)} custom-call(f32[64,128,128]{2,1,0:T(8,128)S(1)} %shard_map.17.buf), custom_call_target="tpu_custom_call" | custom-call | tf_op jit(solution)/shard_map/pallas_call | solution.py:177

commit v2 on v1

v2 whole, which is shorter than its diff:
```python
import jax
import jax.numpy as jnp
from jax import lax
from jax.experimental import pallas as pl
from jax.experimental.pallas import tpu as pltpu
from jax.sharding import PartitionSpec as P

MESH = pl.DeviceIdType.MESH
LANES = 128
ROWS = 128
N = 64
GROUPS = 4
HALF = ROWS // 2
PLANE = [(0, w // 4, w // 2 % 2, w % 2) for w in range(1, 16)]
LINE = [(i, 0, 0, k) for k in range(2) for i in range(1, 4)]
NEAR = PLANE + LINE
STEP = 4


def order():
    first = [(0, 0, 0, 0), (1, 0, 0, 0), (2, 0, 0, 0), (3, 0, 0, 0)]
    first += [(0, 0, 1, 0), (0, 1, 0, 0), (0, 3, 0, 0), (0, 2, 0, 0)]
    first += [(0, 0, 0, 1), (1, 0, 0, 1), (2, 0, 0, 1), (3, 0, 0, 1)]
    near = [o for o in PLANE if o not in first]
    far = [[(1 + k, w // 4, w // 2 % 2, w % 2) for w in range(2, 16)] for k in range(3)]
    rest = []
    for i in range(14):
        rest += [far[k][(5 * i + 4 * k) % 14] for k in range(3)]
        if i * 10 // 14 != (i + 1) * 10 // 14:
            rest.append(near[(3 * len(rest) // 5) % len(near)])
            near.remove(rest[-1])
    return first + rest


ORDER = order()
NOW = 12
TOTAL_AT = 6


def pick(i, values):
    r = values[0]
    for k, v in enumerate(values[1:], 1):
        r = jnp.where(i == k, v, r)
    return r


def split3(v):
    hi = v.astype(jnp.bfloat16)
    rest = v - hi.astype(jnp.float32)
    mid = rest.astype(jnp.bfloat16)
    lo = (rest - mid.astype(jnp.float32)).astype(jnp.bfloat16)
    return hi, mid, lo


def dot(a, b):
    return jnp.dot(a, b, preferred_element_type=jnp.float32)


def gather_kernel(
    x_hbm, buf, xv, lane_w, row_w, part, starts, tot, trecv,
    load_sem, send_sem, recv_sem, tot_send, tot_recv, row_sem, ready_sem,
):
    me = lax.axis_index("dev")
    grp = lax.axis_index("grp")
    y, x, z, c = me // 16, (me // 4) % 4, (me // 2) % 2, me % 2

    def remote(src, dst, ssem, rsem, dev):
        return pltpu.make_async_remote_copy(
            src_ref=src, dst_ref=dst, send_sem=ssem, recv_sem=rsem,
            device_id={"dev": dev}, device_id_type=MESH,
        )

    loads = []
    for i in range(4):
        ts = pl.ds(((y + i) % 4) * 16, 16)
        loads.append(pltpu.make_async_copy(x_hbm.at[ts], xv.at[ts, pl.ds(0, ROWS)], load_sem.at[i]))
        loads[-1].start()
    barrier = pltpu.get_barrier_semaphore()

    def device(o, sign=1):
        return (
            ((y + sign * o[0] + 4) % 4) * 16
            + ((x + sign * o[1] + 4) % 4) * 4
            + ((z + o[2]) % 2) * 2
            + (c + o[3]) % 2
        )

    for o in NEAR:
        pl.semaphore_signal(barrier, inc=1, device_id={"dev": device(o)}, device_id_type=MESH)

    def greet(g, _):
        pl.semaphore_signal(barrier, inc=1, device_id={"grp": g}, device_id_type=MESH)
        return 0

    lax.fori_loop(grp + 1, GROUPS, greet, 0)

    r = lax.broadcasted_iota(jnp.int32, (2 * LANES, 2 * LANES), 0) % LANES
    q = lax.broadcasted_iota(jnp.int32, (2 * LANES, 2 * LANES), 1)
    lane_w[...] = ((r < q) | (q >= LANES)).astype(jnp.float32).astype(jnp.bfloat16)
    r = lax.broadcasted_iota(jnp.int32, (ROWS, 2 * ROWS), 0)
    q = lax.broadcasted_iota(jnp.int32, (ROWS, 2 * ROWS), 1) % ROWS
    row_w[...] = (q < r).astype(jnp.float32).astype(jnp.bfloat16)

    def scan(ts):
        v = jnp.concatenate([xv[t, 0:ROWS] for t in ts], axis=0)
        hi, mid, lo = split3(v)
        both = dot(jnp.concatenate([hi, mid], axis=1), lane_w[...]) + dot(lo, lane_w[0:LANES])
        out = []
        for k in range(len(ts)):
            rows = slice(k * ROWS, (k + 1) * ROWS)
            a, b, d = split3(both[rows, LANES:])
            before = dot(row_w[...], jnp.concatenate([a, b], axis=0)) + dot(row_w[:, 0:ROWS], d)
            out.append(both[rows, :LANES] + before)
        for t, v in zip(ts, out):
            xv[t, 0:ROWS] = v

    def send(t, first, rows):
        rows = pl.ds(first, rows)
        remote(xv.at[t, rows], buf.at[me, rows], send_sem, recv_sem.at[me], t).start()

    for load in loads:
        load.wait()

    def range_sum(t, _):
        part[t] = jnp.sum(xv[t, 0:ROWS].reshape(ROWS // 8, 8, LANES), axis=0)
        return 0

    lax.fori_loop(0, N, range_sum, 0)
    scan([device(o) for o in ORDER[0:STEP]])
    sums = jnp.sum(jnp.sum(part[...], axis=1), axis=1, keepdims=True)
    sums = jnp.broadcast_to(sums, (N, LANES))
    tot[...] = jnp.broadcast_to(jnp.sum(sums, axis=0, keepdims=True), (8, LANES))
    low = row_w[0:N, 0:N]
    a, b, d = split3(sums)
    starts[...] = dot(low, a) + dot(low, b) + dot(low, d)

    pl.semaphore_wait(barrier, len(NEAR) + grp)
    def ready(g, _):
        pl.semaphore_signal(ready_sem, inc=1, device_id={"grp": g}, device_id_type=MESH)
        return 0

    lax.fori_loop(0, grp, ready, 0)
    for i in range(1, 4):
        pl.semaphore_signal(
            row_sem, inc=1, device_id={"dev": device((i, 0, 0, 0))}, device_id_type=MESH
        )
    for o in ORDER[1:STEP]:
        send(device(o), 0, HALF)
    for i in range(STEP, NOW, STEP):
        ts = [device(o) for o in ORDER[i : i + STEP]]
        scan(ts)
        for t in ts:
            send(t, 0, HALF)

    pl.semaphore_wait(row_sem, 3)

    table = [[o[k] for o in ORDER] for k in range(4)]

    def offset(i, m):
        return [pick(i, values[m::STEP]) for values in table]

    def targets(i):
        return [device(offset(i, m)) for m in range(STEP)]

    def scan_and_send(i, _):
        ts = targets(i)
        scan(ts)
        for t in ts:
            send(t, 0, HALF)
        return 0

    lax.fori_loop(NOW // STEP, TOTAL_AT, scan_and_send, 0)

    def send_total(g, _):
        pltpu.make_async_remote_copy(
            src_ref=tot, dst_ref=trecv.at[grp], send_sem=tot_send.at[g], recv_sem=tot_recv.at[grp],
            device_id={"grp": g}, device_id_type=MESH,
        ).start()
        return 0

    @pl.when(grp < GROUPS - 1)
    def _():
        pl.semaphore_wait(ready_sem, GROUPS - 1 - grp)

    lax.fori_loop(grp + 1, GROUPS, send_total, 0)

    lax.fori_loop(TOTAL_AT, N // STEP, scan_and_send, 0)

    def add_total(g, base):
        pltpu.make_async_copy(tot, tot, tot_recv.at[g]).wait()
        return base + trecv[g]

    base = lax.fori_loop(0, grp, add_total, jnp.zeros((8, LANES), jnp.float32))

    def put_start(t, _):
        start = starts[pl.ds(t, 1)] + base[0:1]
        xv[t, HALF:ROWS] += start
        xv[t, ROWS:] = jnp.broadcast_to(start, (8, LANES))
        return 0

    lax.fori_loop(0, N, put_start, 0)
    for o in ORDER[1:]:
        send(device(o), HALF, HALF + 1)
    buf[me, 0:HALF] = xv[me, 0:HALF] + xv[me, ROWS : ROWS + 1]
    buf[me, HALF:ROWS] = xv[me, HALF:ROWS]

    def receive(src):
        slab = buf.at[src, pl.ds(0, ROWS + 1)]
        pltpu.make_async_copy(slab, slab, recv_sem.at[src]).wait()
        buf[src, 0:HALF] += buf[src, ROWS : ROWS + 1]

    for o in ORDER[1:]:
        receive(device(o, -1))

    def total_sent(g, _):
        pltpu.make_async_copy(tot, tot, tot_send.at[g]).wait()
        return 0

    lax.fori_loop(grp + 1, GROUPS, total_sent, 0)
    sent = buf.at[pl.ds(0, N - 1), pl.ds(0, ROWS + 1)]
    pltpu.make_async_copy(sent, sent, send_sem).wait()


def place_kernel(buf, out, sem):
    for t in range(N):
        pltpu.make_async_copy(buf.at[t, pl.ds(0, ROWS)], out.at[t // 8, :, t % 8], sem).start()
    pltpu.make_async_copy(out, out, sem).wait()


def local(amounts):
    slabs = amounts.reshape(N, ROWS, LANES)
    f32, bf16, dma = jnp.float32, jnp.bfloat16, pltpu.SemaphoreType.DMA
    buf = pl.pallas_call(
        gather_kernel,
        out_shape=pltpu.VMEM((N, ROWS + 8, LANES), f32),
        in_specs=[pl.BlockSpec(memory_space=pltpu.HBM)],
        out_specs=pl.BlockSpec(memory_space=pltpu.VMEM),
        scratch_shapes=[
            pltpu.VMEM((N, ROWS + 8, LANES), f32),
            pltpu.VMEM((2 * LANES, 2 * LANES), bf16),
            pltpu.VMEM((ROWS, 2 * ROWS), bf16),
            pltpu.VMEM((N, 8, LANES), f32),
            pltpu.VMEM((N, LANES), f32),
            pltpu.VMEM((8, LANES), f32),
            pltpu.VMEM((GROUPS, 8, LANES), f32),
            dma((4,)), dma, dma((N,)), dma((GROUPS,)), dma((GROUPS,)),
            pltpu.SemaphoreType.REGULAR, pltpu.SemaphoreType.REGULAR,
        ],
        compiler_params=pltpu.CompilerParams(
            collective_id=0, has_side_effects=True, vmem_limit_bytes=56 * 2**20
        ),
    )(slabs)
    out = pl.pallas_call(
        place_kernel,
        out_shape=jax.ShapeDtypeStruct((8, ROWS, 8, LANES), f32),
        in_specs=[pl.BlockSpec(memory_space=pltpu.VMEM)],
        out_specs=pl.BlockSpec(memory_space=pltpu.HBM),
        scratch_shapes=[dma],
        compiler_params=pltpu.CompilerParams(vmem_limit_bytes=8 * 2**20),
    )(pltpu.with_memory_space_constraint(buf, pltpu.VMEM))
    return out.transpose(0, 2, 1, 3).reshape(N, ROWS * LANES)


def solution(mesh):
    return jax.shard_map(
        local,
        mesh=mesh,
        in_specs=(P("dev", "grp"),),
        out_specs=P(None, ("grp", "dev")),
        check_vma=False,
    )
```

time: 76.4 us -> 61.6 us (0.81)
  the two profiles are of different devices: /device:TPU:41 before, /device:TPU:1 now
where the time goes in v2:
time: 61.6 us; the launch traced here: 61.5 us
  Pallas kernels  61.5 us (100%)
    pallas_call x1, Pallas kernels, local(): pl.pallas_call(gather_kernel, out_shape=pltpu.VMEM((N, ROWS + 8, LANES),...  59.6 us
    pallas_call x1, Pallas kernels, local(): pl.pallas_call(place_kernel, out_shape=jax.ShapeDtypeStruct((8, ROWS, 8,...  1.97 us

profile of v2, /device:TPU:1, one launch (start us, length us, event | category | flops | bytes accessed | tf_op | source)
XLA Modules:
  0.0 61.5 jit_solution(13688965090630235011)
XLA Ops:
  0.0 59.6 %shard_map.17.buf = f32[64,136,128]{2,1,0:T(8,128)S(1)} custom-call(f32[64,128,128]{2,1,0:T(8,128)} %bitcast.4), custom_call_target="tpu_custom_call" | custom-call | tf_op jit(solution)/shard_map/pallas_call | solution.py:233
  59.6 2.0 %shard_map.18 = f32[8,128,8,128]{3,2,1,0:T(8,128)} custom-call(f32[64,136,128]{2,1,0:T(8,128)S(1)} %shard_map.17.buf), custom_call_target="tpu_custom_call" | custom-call | tf_op jit(solution)/shard_map/pallas_call | solution.py:253

commit v3 on v2

v3 whole, which is shorter than its diff:
```python
import jax
import jax.numpy as jnp
from jax import lax
from jax.experimental import pallas as pl
from jax.experimental.pallas import tpu as pltpu
from jax.sharding import PartitionSpec as P

MESH = pl.DeviceIdType.MESH
LANES = 128
ROWS = 128
N = 64
GROUPS = 4
HALF = ROWS // 2
PLANE = [(0, w // 4, w // 2 % 2, w % 2) for w in range(1, 16)]
LINE = [(i, 0, 0, k) for k in range(2) for i in range(1, 4)]
NEAR = PLANE + LINE
STEP = 4


def order():
    first = [(0, 0, 0, 0), (0, 0, 1, 0), (0, 1, 0, 0), (0, 3, 0, 0)]
    first += [(1, 0, 0, 0), (3, 0, 0, 0), (0, 0, 1, 1), (0, 1, 0, 1)]
    first += [(0, 3, 0, 1), (1, 0, 0, 1), (3, 0, 0, 1), (0, 0, 0, 1)]
    near = [o for o in NEAR if o not in first]
    far = [[(1 + k, w // 4, w // 2 % 2, w % 2) for w in range(2, 16)] for k in range(3)]
    rest = []
    for i in range(14):
        rest += [far[k][(5 * i + 4 * k) % 14] for k in range(3)]
        if i * 10 // 14 != (i + 1) * 10 // 14:
            rest.append(near[(3 * len(rest) // 5) % len(near)])
            near.remove(rest[-1])
    return first + rest


ORDER = order()
NOW = 12
SOON = 36


def pick(i, values):
    r = values[0]
    for k, v in enumerate(values[1:], 1):
        r = jnp.where(i == k, v, r)
    return r


def split3(v):
    hi = v.astype(jnp.bfloat16)
    rest = v - hi.astype(jnp.float32)
    mid = rest.astype(jnp.bfloat16)
    lo = (rest - mid.astype(jnp.float32)).astype(jnp.bfloat16)
    return hi, mid, lo


def dot(a, b):
    return jnp.dot(a, b, preferred_element_type=jnp.float32)


def gather_kernel(
    x_hbm, buf, xr, xv, lane_w, row_w, part, starts, halves, tot, trecv,
    load_sem, send_sem, first_sem, second_sem, tot_send, tot_recv, row_sem, ready_sem,
):
    me = lax.axis_index("dev")
    grp = lax.axis_index("grp")
    y, x, z, c = me // 16, (me // 4) % 4, (me // 2) % 2, me % 2

    def remote(src, dst, ssem, rsem, dev):
        return pltpu.make_async_remote_copy(
            src_ref=src, dst_ref=dst, send_sem=ssem, recv_sem=rsem,
            device_id={"dev": dev}, device_id_type=MESH,
        )

    loads = []
    for i in range(4):
        ts = pl.ds(((y + i) % 4) * 16, 16)
        loads.append(pltpu.make_async_copy(x_hbm.at[ts], xr.at[ts], load_sem.at[i]))
        loads[-1].start()
    barrier = pltpu.get_barrier_semaphore()

    def device(o, sign=1):
        return (
            ((y + sign * o[0] + 4) % 4) * 16
            + ((x + sign * o[1] + 4) % 4) * 4
            + ((z + o[2]) % 2) * 2
            + (c + o[3]) % 2
        )

    for o in NEAR:
        pl.semaphore_signal(barrier, inc=1, device_id={"dev": device(o)}, device_id_type=MESH)

    def greet(g, _):
        pl.semaphore_signal(barrier, inc=1, device_id={"grp": g}, device_id_type=MESH)
        return 0

    lax.fori_loop(grp + 1, GROUPS, greet, 0)

    pl.semaphore_wait(barrier, len(NEAR) + grp)
    for i in range(1, 4):
        pl.semaphore_signal(
            row_sem, inc=1, device_id={"dev": device((i, 0, 0, 0))}, device_id_type=MESH
        )

    def send_first(order):
        half = pl.ds(0, HALF)
        for o in order:
            t = device(o)
            remote(x_hbm.at[t, half], buf.at[me, half], send_sem, first_sem.at[me], t).start()

    send_first(ORDER[1:NOW])

    def ready(g, _):
        pl.semaphore_signal(ready_sem, inc=1, device_id={"grp": g}, device_id_type=MESH)
        return 0

    lax.fori_loop(0, grp, ready, 0)

    r = lax.broadcasted_iota(jnp.int32, (2 * LANES, 2 * LANES), 0) % LANES
    q = lax.broadcasted_iota(jnp.int32, (2 * LANES, 2 * LANES), 1)
    lane_w[...] = ((r < q) | (q >= LANES)).astype(jnp.float32).astype(jnp.bfloat16)
    r = lax.broadcasted_iota(jnp.int32, (ROWS, 2 * ROWS), 0)
    q = lax.broadcasted_iota(jnp.int32, (ROWS, 2 * ROWS), 1) % ROWS
    row_w[...] = (q < r).astype(jnp.float32).astype(jnp.bfloat16)

    def lane_scan(v):
        hi, mid, lo = split3(v)
        return dot(jnp.concatenate([hi, mid], axis=1), lane_w[...]) + dot(lo, lane_w[0:LANES])

    def scan(ts):
        both = lane_scan(jnp.concatenate([xr[t] for t in ts], axis=0))
        out = []
        for k in range(len(ts)):
            rows = slice(k * ROWS, (k + 1) * ROWS)
            a, b, d = split3(both[rows, LANES:])
            before = dot(row_w[...], jnp.concatenate([a, b], axis=0)) + dot(row_w[:, 0:ROWS], d)
            out.append(both[rows, :LANES] + before)
        for t, v in zip(ts, out):
            xv[t] = v

    pl.semaphore_wait(row_sem, 3)
    send_first(ORDER[NOW:SOON])
    for load in loads:
        load.wait()

    def range_sum(t, _):
        part[t] = jnp.sum(xr[t].reshape(ROWS // 8, 8, LANES), axis=0)
        return 0

    lax.fori_loop(0, N, range_sum, 0)
    sums = jnp.sum(jnp.sum(part[...], axis=1), axis=1, keepdims=True)
    sums = jnp.broadcast_to(sums, (N, LANES))
    tot[...] = jnp.broadcast_to(jnp.sum(sums, axis=0, keepdims=True), (8, LANES))
    low = row_w[0:N, 0:N]
    a, b, d = split3(sums)
    starts[...] = dot(low, a) + dot(low, b) + dot(low, d)

    @pl.when(grp < GROUPS - 1)
    def _():
        pl.semaphore_wait(ready_sem, GROUPS - 1 - grp)

    def send_total(g, _):
        pltpu.make_async_remote_copy(
            src_ref=tot, dst_ref=trecv.at[grp], send_sem=tot_send.at[g], recv_sem=tot_recv.at[grp],
            device_id={"grp": g}, device_id_type=MESH,
        ).start()
        return 0

    lax.fori_loop(grp + 1, GROUPS, send_total, 0)
    send_first(ORDER[SOON:])

    table = [[o[k] for o in ORDER] for k in range(4)]

    def devices(i, sign=1):
        return [device([pick(i, v[m::STEP]) for v in table], sign) for m in range(STEP)]

    def scan_step(i, _):
        scan(devices(i))
        return 0

    lax.fori_loop(0, N // STEP, scan_step, 0)

    def add_total(g, base):
        pltpu.make_async_copy(tot, tot, tot_recv.at[g]).wait()
        return base + trecv[g]

    base = lax.fori_loop(0, grp, add_total, jnp.zeros((8, LANES), jnp.float32))

    def put_start(t, _):
        xv[t] += starts[pl.ds(t, 1)] + base[0:1]
        return 0

    lax.fori_loop(0, N, put_start, 0)
    for o in ORDER[1:]:
        t, half = device(o), pl.ds(HALF, HALF)
        remote(xv.at[t, half], buf.at[me, half], send_sem, second_sem.at[me], t).start()
    buf[me] = xv[me]

    low_half = row_w[0:HALF, 0:HALF]

    def scan_first(srcs):
        for src in srcs:
            half = buf.at[src, pl.ds(0, HALF)]
            pltpu.make_async_copy(half, half, first_sem.at[src]).wait()
        both = lane_scan(jnp.concatenate([buf[src, 0:HALF] for src in srcs], axis=0))
        out = []
        for k in range(len(srcs)):
            rows = slice(k * HALF, (k + 1) * HALF)
            sums = both[rows, LANES:]
            a, b, d = split3(sums)
            before = dot(low_half, a) + dot(low_half, b) + dot(low_half, d)
            out.append((both[rows, :LANES] + before, (before + sums)[HALF - 1 :]))
        for src, (v, total) in zip(srcs, out):
            buf[src, 0:HALF] = v
            halves[pl.ds(src, 1)] = total

    scan_first([device(o, -1) for o in ORDER[1:STEP]])

    def first_step(i, _):
        scan_first(devices(i, -1))
        return 0

    lax.fori_loop(1, N // STEP, first_step, 0)

    for o in ORDER[1:]:
        src = device(o, -1)
        half = buf.at[src, pl.ds(HALF, HALF)]
        pltpu.make_async_copy(half, half, second_sem.at[src]).wait()
        start = jnp.broadcast_to(buf[src, HALF : HALF + 1, 0:1], (1, LANES)) - halves[pl.ds(src, 1)]
        buf[src, 0:HALF] += start

    def total_sent(g, _):
        pltpu.make_async_copy(tot, tot, tot_send.at[g]).wait()
        return 0

    lax.fori_loop(grp + 1, GROUPS, total_sent, 0)
    sent = buf.at[pl.ds(0, N - 1)]
    pltpu.make_async_copy(sent, sent, send_sem).wait()


def place_kernel(buf, out, sem):
    for t in range(N):
        pltpu.make_async_copy(buf.at[t], out.at[t // 8, :, t % 8], sem).start()
    pltpu.make_async_copy(out, out, sem).wait()


def local(amounts):
    slabs = amounts.reshape(N, ROWS, LANES)
    f32, bf16, dma = jnp.float32, jnp.bfloat16, pltpu.SemaphoreType.DMA
    buf = pl.pallas_call(
        gather_kernel,
        out_shape=pltpu.VMEM((N, ROWS, LANES), f32),
        in_specs=[pl.BlockSpec(memory_space=pltpu.HBM)],
        out_specs=pl.BlockSpec(memory_space=pltpu.VMEM),
        scratch_shapes=[
            pltpu.VMEM((N, ROWS, LANES), f32),
            pltpu.VMEM((N, ROWS, LANES), f32),
            pltpu.VMEM((2 * LANES, 2 * LANES), bf16),
            pltpu.VMEM((ROWS, 2 * ROWS), bf16),
            pltpu.VMEM((N, 8, LANES), f32),
            pltpu.VMEM((N, LANES), f32),
            pltpu.VMEM((N, LANES), f32),
            pltpu.VMEM((8, LANES), f32),
            pltpu.VMEM((GROUPS, 8, LANES), f32),
            dma((4,)), dma, dma((N,)), dma((N,)), dma((GROUPS,)), dma((GROUPS,)),
            pltpu.SemaphoreType.REGULAR, pltpu.SemaphoreType.REGULAR,
        ],
        compiler_params=pltpu.CompilerParams(
            collective_id=0, has_side_effects=True, vmem_limit_bytes=56 * 2**20
        ),
    )(slabs)
    out = pl.pallas_call(
        place_kernel,
        out_shape=jax.ShapeDtypeStruct((8, ROWS, 8, LANES), f32),
        in_specs=[pl.BlockSpec(memory_space=pltpu.VMEM)],
        out_specs=pl.BlockSpec(memory_space=pltpu.HBM),
        scratch_shapes=[dma],
        compiler_params=pltpu.CompilerParams(vmem_limit_bytes=8 * 2**20),
    )(pltpu.with_memory_space_constraint(buf, pltpu.VMEM))
    return out.transpose(0, 2, 1, 3).reshape(N, ROWS * LANES)


def solution(mesh):
    return jax.shard_map(
        local,
        mesh=mesh,
        in_specs=(P("dev", "grp"),),
        out_specs=P(None, ("grp", "dev")),
        check_vma=False,
    )
```

time: 61.6 us -> 59.8 us (0.971)
  Pallas kernels: 61.5 us -> 59.5 us
    pallas_call x1, Pallas kernels: 59.6 us -> 57.6 us  [local(): pl.pallas_call(gather_kernel, out_shape=pltpu.VMEM((N, ROWS, LANES), f32)...]
where the time goes in v3:
time: 59.8 us; the launch traced here: 59.5 us
  Pallas kernels  59.5 us (99%)
    pallas_call x1, Pallas kernels, local(): pl.pallas_call(gather_kernel, out_shape=pltpu.VMEM((N, ROWS, LANES), f32)...  57.6 us
    pallas_call x1, Pallas kernels, local(): pl.pallas_call(place_kernel, out_shape=jax.ShapeDtypeStruct((8, ROWS, 8,...  1.97 us

profile of v3, /device:TPU:1, one launch (start us, length us, event | category | flops | bytes accessed | tf_op | source)
XLA Modules:
  0.0 59.5 jit_solution(10907331445956179831)
XLA Ops:
  0.0 57.6 %shard_map.17.buf = f32[64,128,128]{2,1,0:T(8,128)S(1)} custom-call(f32[64,128,128]{2,1,0:T(8,128)} %bitcast.4), custom_call_target="tpu_custom_call" | custom-call | tf_op jit(solution)/shard_map/pallas_call | solution.py:248
  57.6 2.0 %shard_map.18 = f32[8,128,8,128]{3,2,1,0:T(8,128)} custom-call(f32[64,128,128]{2,1,0:T(8,128)S(1)} %shard_map.17.buf), custom_call_target="tpu_custom_call" | custom-call | tf_op jit(solution)/shard_map/pallas_call | solution.py:270

commit v4 on v3

--- a/solution.py
+++ b/solution.py
@@ -18,17 +18,18 @@
 
 
 def order():
-    first = [(0, 0, 0, 0), (0, 0, 1, 0), (0, 1, 0, 0), (0, 3, 0, 0)]
-    first += [(1, 0, 0, 0), (3, 0, 0, 0), (0, 0, 1, 1), (0, 1, 0, 1)]
-    first += [(0, 3, 0, 1), (1, 0, 0, 1), (3, 0, 0, 1), (0, 0, 0, 1)]
-    near = [o for o in NEAR if o not in first]
+    first = [(0, 0, 0, 0)]
+    for k in range(2):
+        first += [(0, 0, 1, k), (0, 1, 0, k), (1, 0, 0, k), (0, 3, 0, k), (3, 0, 0, k)]
+    first.append((0, 0, 0, 1))
+    near = [(2, 0, 0, 0), (0, 2, 0, 0), (2, 0, 0, 1), (0, 1, 1, 1), (0, 3, 1, 0)]
+    near += [(0, 2, 1, 0), (0, 2, 0, 1), (0, 1, 1, 0), (0, 3, 1, 1), (0, 2, 1, 1)]
     far = [[(1 + k, w // 4, w // 2 % 2, w % 2) for w in range(2, 16)] for k in range(3)]
     rest = []
     for i in range(14):
-        rest += [far[k][(5 * i + 4 * k) % 14] for k in range(3)]
+        rest += [far[k][(5 * i + 4 * k + 3) % 14] for k in range(3)]
         if i * 10 // 14 != (i + 1) * 10 // 14:
-            rest.append(near[(3 * len(rest) // 5) % len(near)])
-            near.remove(rest[-1])
+            rest.append(near.pop((3 * len(rest) // 5) % len(near)))
     return first + rest
 
 

time: 59.8 us -> 58.6 us (0.980)
  Pallas kernels: 59.5 us -> 58.5 us
    pallas_call x1, Pallas kernels: 57.6 us -> 56.6 us  [local(): pl.pallas_call(gather_kernel, out_shape=pltpu.VMEM((N, ROWS, LANES), f32)...]
where the time goes in v4:
time: 58.6 us; the launch traced here: 58.5 us
  Pallas kernels  58.5 us (100%)
    pallas_call x1, Pallas kernels, local(): pl.pallas_call(gather_kernel, out_shape=pltpu.VMEM((N, ROWS, LANES), f32)...  56.6 us
    pallas_call x1, Pallas kernels, local(): pl.pallas_call(place_kernel, out_shape=jax.ShapeDtypeStruct((8, ROWS, 8,...  1.97 us

profile of v4, /device:TPU:1, one launch (start us, length us, event | category | flops | bytes accessed | tf_op | source)
XLA Modules:
  0.0 58.5 jit_solution(15087348537903696458)
XLA Ops:
  0.0 56.6 %shard_map.17.buf = f32[64,128,128]{2,1,0:T(8,128)S(1)} custom-call(f32[64,128,128]{2,1,0:T(8,128)} %bitcast.4), custom_call_target="tpu_custom_call" | custom-call | tf_op jit(solution)/shard_map/pallas_call | solution.py:249
  56.6 2.0 %shard_map.18 = f32[8,128,8,128]{3,2,1,0:T(8,128)} custom-call(f32[64,128,128]{2,1,0:T(8,128)S(1)} %shard_map.17.buf), custom_call_target="tpu_custom_call" | custom-call | tf_op jit(solution)/shard_map/pallas_call | solution.py:271

commit v5 on v4

--- a/solution.py
+++ b/solution.py
@@ -13,8 +13,9 @@
 HALF = ROWS // 2
 PLANE = [(0, w // 4, w // 2 % 2, w % 2) for w in range(1, 16)]
 LINE = [(i, 0, 0, k) for k in range(2) for i in range(1, 4)]
-NEAR = PLANE + LINE
+NEAR = PLANE[::-1] + LINE
 STEP = 4
+LAST = 8
 
 
 def order():
@@ -71,11 +72,6 @@
             device_id={"dev": dev}, device_id_type=MESH,
         )
 
-    loads = []
-    for i in range(4):
-        ts = pl.ds(((y + i) % 4) * 16, 16)
-        loads.append(pltpu.make_async_copy(x_hbm.at[ts], xr.at[ts], load_sem.at[i]))
-        loads[-1].start()
     barrier = pltpu.get_barrier_semaphore()
 
     def device(o, sign=1):
@@ -94,6 +90,11 @@
         return 0
 
     lax.fori_loop(grp + 1, GROUPS, greet, 0)
+    loads = []
+    for i in range(4):
+        ts = pl.ds(((y + i) % 4) * 16, 16)
+        loads.append(pltpu.make_async_copy(x_hbm.at[ts], xr.at[ts], load_sem.at[i]))
+        loads[-1].start()
 
     pl.semaphore_wait(barrier, len(NEAR) + grp)
     for i in range(1, 4):
@@ -221,12 +222,15 @@
 
     lax.fori_loop(1, N // STEP, first_step, 0)
 
-    for o in ORDER[1:]:
-        src = device(o, -1)
-        half = buf.at[src, pl.ds(HALF, HALF)]
-        pltpu.make_async_copy(half, half, second_sem.at[src]).wait()
-        start = jnp.broadcast_to(buf[src, HALF : HALF + 1, 0:1], (1, LANES)) - halves[pl.ds(src, 1)]
-        buf[src, 0:HALF] += start
+    for i in range(0, N, LAST):
+        srcs = [device(o, -1) for o in ORDER[max(i, 1) : i + LAST]]
+        for src in srcs:
+            half = buf.at[src, pl.ds(HALF, HALF)]
+            pltpu.make_async_copy(half, half, second_sem.at[src]).wait()
+        heads = [jnp.broadcast_to(buf[src, HALF : HALF + 1, 0:1], (1, LANES)) for src in srcs]
+        out = [buf[src, 0:HALF] + (h - halves[pl.ds(src, 1)]) for src, h in zip(srcs, heads)]
+        for src, v in zip(srcs, out):
+            buf[src, 0:HALF] = v
 
     def total_sent(g, _):
         pltpu.make_async_copy(tot, tot, tot_send.at[g]).wait()

time: 58.6 us -> 58.2 us (level)
  no operation moved by 1% of the time
where the time goes in v5:
time: 58.2 us; the launch traced here: 58.1 us
  Pallas kernels  58.1 us (100%)
    pallas_call x1, Pallas kernels, local(): pl.pallas_call(gather_kernel, out_shape=pltpu.VMEM((N, ROWS, LANES), f32)...  56.2 us
    pallas_call x1, Pallas kernels, local(): pl.pallas_call(place_kernel, out_shape=jax.ShapeDtypeStruct((8, ROWS, 8,...  1.97 us

profile of v5, /device:TPU:1, one launch (start us, length us, event | category | flops | bytes accessed | tf_op | source)
XLA Modules:
  0.0 58.1 jit_solution(1587045566674613779)
XLA Ops:
  0.0 56.2 %shard_map.17.buf = f32[64,128,128]{2,1,0:T(8,128)S(1)} custom-call(f32[64,128,128]{2,1,0:T(8,128)} %bitcast.4), custom_call_target="tpu_custom_call" | custom-call | tf_op jit(solution)/shard_map/pallas_call | solution.py:253
  56.2 2.0 %shard_map.18 = f32[8,128,8,128]{3,2,1,0:T(8,128)} custom-call(f32[64,128,128]{2,1,0:T(8,128)S(1)} %shard_map.17.buf), custom_call_target="tpu_custom_call" | custom-call | tf_op jit(solution)/shard_map/pallas_call | solution.py:275

commit v6 on v5

--- a/solution.py
+++ b/solution.py
@@ -138,8 +138,6 @@
         for t, v in zip(ts, out):
             xv[t] = v
 
-    pl.semaphore_wait(row_sem, 3)
-    send_first(ORDER[NOW:SOON])
     for load in loads:
         load.wait()
 
@@ -154,6 +152,9 @@
     low = row_w[0:N, 0:N]
     a, b, d = split3(sums)
     starts[...] = dot(low, a) + dot(low, b) + dot(low, d)
+
+    pl.semaphore_wait(row_sem, 3)
+    send_first(ORDER[NOW:SOON])
 
     @pl.when(grp < GROUPS - 1)
     def _():

time: 58.2 us -> 58.1 us (level)
  no operation moved by 1% of the time
where the time goes in v6:
time: 58.1 us; the launch traced here: 58 us
  Pallas kernels  58 us (100%)
    pallas_call x1, Pallas kernels, local(): pl.pallas_call(gather_kernel, out_shape=pltpu.VMEM((N, ROWS, LANES), f32)...  56.1 us
    pallas_call x1, Pallas kernels, local(): pl.pallas_call(place_kernel, out_shape=jax.ShapeDtypeStruct((8, ROWS, 8,...  1.97 us

profile of v6, /device:TPU:1, one launch (start us, length us, event | category | flops | bytes accessed | tf_op | source)
XLA Modules:
  0.0 58.0 jit_solution(13559480540949988647)
XLA Ops:
  0.0 56.1 %shard_map.17.buf = f32[64,128,128]{2,1,0:T(8,128)S(1)} custom-call(f32[64,128,128]{2,1,0:T(8,128)} %bitcast.4), custom_call_target="tpu_custom_call" | custom-call | tf_op jit(solution)/shard_map/pallas_call | solution.py:254
  56.1 2.0 %shard_map.18 = f32[8,128,8,128]{3,2,1,0:T(8,128)} custom-call(f32[64,128,128]{2,1,0:T(8,128)S(1)} %shard_map.17.buf), custom_call_target="tpu_custom_call" | custom-call | tf_op jit(solution)/shard_map/pallas_call | solution.py:276
